TPU v7x, 32 devices: a whole 2x2x4 slice. The times are simulated.
32 devices in a mesh: ice: 4 (over x, core), ocn: 8 (over z, y).
Axes of the slice: x: 2, y: 2, z: 4, core: 2. Of those that a mesh axis runs over, the one named last changes fastest.
Arguments:
- ice_state: bfloat16 [5, 20, 32768], P(None, None, ('ice', 'ocn')), may hold values from -6 to 6
- ocean_state: bfloat16 [5, 20, 32768], P(None, None, ('ice', 'ocn')), may hold values from -5 to 5
- ice_rate: float32 [5, 20], replicated, may hold values from 0.2 to 2
- block_weights: bfloat16 [1024, 128, 128], P(('ice', 'ocn')), may hold values from -0.375 to 0.375
- block_route: int32 [1024, 1], P(('ice', 'ocn')), may hold values from 0 to 31; in each aligned block of 32 rows (0 to 31, 32 to 63, ...) at most 2 rows name the same one
- block_tiles: int32 [1024, 2], P(('ice', 'ocn')), may hold values from 0 to 7
- block_valid: int32 [1024], P(('ice', 'ocn')), may hold values from 16 to 128
- ice_mask: int32 [32768], P(('ice', 'ocn')), may hold values 0 or 1
Outputs:
- ice_final: bfloat16 [5, 20, 32768], P(None, None, ('ice', 'ocn'))
- ocean_flux: bfloat16 [5, 20, 32768], P(None, None, ('ice', 'ocn'))
Inputs may be any that keep to these rules, and one draw needn't show every extreme that they name: `block_route`: among the blocks of one device no destination appears more than 2 times.
All inputs are finite; a program needn't handle non-finite values. No bound on the sum of `ice_mask` on one device may be relied on, other than what follows from the above.
Results may differ from a plain program's by a relative error of at most 0.008.
Values may be sent and summed in bfloat16 or wider, within the bound.
A program may use at most 128 MiB of HBM per device.

v0:
```python
import jax
import jax.numpy as jnp
from jax import lax
from jax.sharding import PartitionSpec as P

CAP = 2


def forward_move(buffer):
    return lax.all_to_all(buffer, ("ice", "ocn"), split_axis=0, concat_axis=0, tiled=True)


def back_move(buffer):
    return lax.all_to_all(buffer, ("ice", "ocn"), split_axis=0, concat_axis=0, tiled=True)


def on_device(
    ice_state, ocean_state, ice_rate, block_weights, block_route, block_tiles, block_valid, ice_mask
):
    cats, fields, cells = ice_state.shape
    chans = cats * fields
    blocks, width, unused = block_weights.shape
    tiles = cells // width
    devices = lax.axis_size(("ice", "ocn"))
    route = block_route[:, 0]
    source = block_tiles[:, 0]
    target = block_tiles[:, 1]
    order = jnp.arange(blocks, dtype=jnp.int32)
    earlier = (route[None, :] == route[:, None]) & (order[None, :] < order[:, None])
    slot = jnp.sum(earlier.astype(jnp.int32), axis=1)
    place = route * CAP + slot
    live = jnp.arange(width, dtype=jnp.int32)[None, :] < block_valid[:, None]
    masked = jnp.where(live[:, :, None], block_weights, jnp.zeros((), jnp.bfloat16))
    meta_send = (
        jnp.full((devices * CAP,), -1, jnp.int32).at[place].set(target).reshape(devices, CAP)
    )
    meta = lax.all_to_all(
        meta_send, ("ice", "ocn"), split_axis=0, concat_axis=0, tiled=True
    ).reshape(devices * CAP)
    tile_ids = jnp.arange(tiles, dtype=jnp.int32)
    picker_ocean = (meta[None, :] == tile_ids[:, None]).astype(jnp.bfloat16)
    picker_ice = (source[None, :] == tile_ids[:, None]).astype(jnp.float32)
    rates = ice_rate.reshape(chans, 1)
    land = ice_mask.astype(jnp.float32)[None, :]
    ocean = ocean_state.reshape(chans, cells).astype(jnp.float32)
    ice = (ice_state * ice_mask.astype(jnp.bfloat16)[None, None, :]).reshape(chans, cells)
    flux = ocean_state.reshape(chans, cells)
    for turn in range(2):
        picked = ice.reshape(chans, tiles, width)[:, source, :]
        prods = jnp.einsum(
            "cbi,bio->bco", picked, masked, preferred_element_type=jnp.float32
        ).astype(jnp.bfloat16)
        outgoing = jnp.zeros((devices * CAP, chans, width), jnp.bfloat16).at[place].set(prods)
        arrived = forward_move(outgoing.reshape(devices, CAP, chans, width)).reshape(
            devices * CAP, chans, width
        )
        ocean_in = jnp.einsum(
            "tk,kcj->ctj", picker_ocean, arrived, preferred_element_type=jnp.float32
        ).reshape(chans, cells)
        flux = jnp.tanh(ocean_in + ocean).astype(jnp.bfloat16)
        flux_tiles = flux.reshape(chans, tiles, width)
        replies = jnp.einsum(
            "tk,ctj->kcj", picker_ocean, flux_tiles, preferred_element_type=jnp.float32
        ).astype(jnp.bfloat16)
        returned = back_move(replies.reshape(devices, CAP, chans, width)).reshape(
            devices * CAP, chans, width
        )
        taken = returned[place]
        contrib = jnp.einsum("bco,bio->bci", taken, masked, preferred_element_type=jnp.float32)
        forcing = jnp.einsum(
            "tb,bci->cti", picker_ice, contrib, precision=lax.Precision.HIGHEST
        ).reshape(chans, cells)
        ice = (land * (ice.astype(jnp.float32) + rates * jnp.tanh(forcing))).astype(jnp.bfloat16)
    return (ice.reshape(cats, fields, cells), flux.reshape(cats, fields, cells))


def solution(mesh):
    placed = (
        P(None, None, ("ice", "ocn")),
        P(None, None, ("ice", "ocn")),
        P(),
        P(("ice", "ocn"), None, None),
        P(("ice", "ocn"), None),
        P(("ice", "ocn"), None),
        P(("ice", "ocn")),
        P(("ice", "ocn")),
    )
    return jax.shard_map(
        on_device,
        mesh=mesh,
        in_specs=placed,
        out_specs=(P(None, None, ("ice", "ocn")), P(None, None, ("ice", "ocn"))),
        check_vma=False,
    )
```

profile of v0, /device:TPU:0, one launch (start us, length us, event | category | flops | bytes accessed | tf_op | source)
XLA Modules:
  0.0 230.9 jit_solution(6869753244900772257)
XLA Ops:
  0.6 0.9 convert_reduce_fusion
  1.6 0.8 slice_bitcast_fusion.1
  2.3 0.7 scatter_custom_fusion
  3.0 0.7 all_to_all.18
  3.7 7.3 %all-to-all-start = ((s32[32,1,2]{2,1,0:T(1,128)}), s32[32,1,2]{2,1,0:T(1,128)S(1)}, u32[]{:S(2)}, u32[]{:S(2)}) async-start(s32[32,1,2]{2,1,0:T(1,128)} %bitcast.4), calls=%async_computation | async-start | bytes 32768 | tf_op jit(solution)/shard_map/all_to_all | solution.py:37
  11.1 0.8 fusion.49
  11.8 1.0 broadcast_multiply_fusion
  13.0 0.7 iota_compare_fusion
  13.7 0.7 gather_fusion
  14.5 1.9 convolution_convert_fusion.3
  16.3 0.2 broadcast.57.clone
  16.5 3.5 %scatter_fusion = bf16[64,100,128]{2,1,0:T(8,128)(2,1)S(1)} fusion(bf16[64,100,128]{2,1,0:T(8,128)(2,1)S(1)} %broadcast.57.clone, s32[32]{0:T(128)S(1)} %get-tuple-element.10, bf16[32,100,128]{2,1,0:T(8,128)(2,1)} %convolution_convert_fusion.3), kind=kCustom, calls=%fused_computation.5 | custom fusion | bytes 2457728 | tf_op jit(solution)/shard_map/scatter | solution.py:53
  20.1 2.4 %copy.32 = bf16[32,2,100,128]{3,1,2,0:T(2,128)(2,1)} copy(bf16[32,2,100,128]{3,2,1,0:T(8,128)(2,1)S(1)} %bitcast.68) | data formatting | bytes 3276800 | tf_op jit(solution)/shard_map/reshape | solution.py:54
  22.5 5.8 %all-to-all-start.1 = ((bf16[32,2,100,128]{3,1,2,0:T(2,128)(2,1)}), bf16[32,2,100,128]{3,1,2,0:T(2,128)(2,1)S(1)}, u32[]{:S(2)}, u32[]{:S(2)}) async-start(bf16[32,2,100,128]{3,1,2,0:T(2,128)(2,1)} %copy.32), calls=%async_computation.1 | async-start | bytes 3276800 | tf_op jit(solution)/shard_map/all_to_all | solution.py:10
  28.4 1.1 reshape.122
  29.4 0.5 broadcast.78
  30.0 0.7 reduce.3
  30.8 37.8 %all-to-all-done.1 = bf16[32,2,100,128]{3,1,2,0:T(2,128)(2,1)S(1)} async-done(((bf16[32,2,100,128]{3,1,2,0:T(2,128)(2,1)}), bf16[32,2,100,128]{3,1,2,0:T(2,128)(2,1)S(1)}, u32[]{:S(2)}, u32[]{:S(2)}) %all-to-all-start.1) | async-done | bytes 1638432 | tf_op jit(solution)/shard_map/all_to_all | solution.py:10
  68.6 3.0 %copy.33 = bf16[32,2,100,128]{3,1,0,2:T(2,128)(2,1)} copy(bf16[32,2,100,128]{3,1,2,0:T(2,128)(2,1)S(1)} %all-to-all-done.1) | data formatting | bytes 3276800 | tf_op jit(solution)/shard_map/all_to_all | solution.py:10
  71.6 2.2 convolution_convert_fusion.1
  73.8 2.3 copy.34
  76.1 2.8 %all-to-all-start.2 = ((bf16[32,2,100,128]{3,1,2,0:T(2,128)(2,1)}), bf16[32,2,100,128]{3,1,2,0:T(2,128)(2,1)S(1)}, u32[]{:S(2)}, u32[]{:S(2)}) async-start(bf16[32,2,100,128]{3,1,2,0:T(2,128)(2,1)} %copy.34), calls=%async_computation.2 | async-start | bytes 3276800 | tf_op jit(solution)/shard_map/all_to_all | solution.py:14
  79.0 40.1 %all-to-all-done.2 = bf16[32,2,100,128]{3,1,2,0:T(2,128)(2,1)S(1)} async-done(((bf16[32,2,100,128]{3,1,2,0:T(2,128)(2,1)}), bf16[32,2,100,128]{3,1,2,0:T(2,128)(2,1)S(1)}, u32[]{:S(2)}, u32[]{:S(2)}) %all-to-all-start.2) | async-done | bytes 1638432 | tf_op jit(solution)/shard_map/all_to_all | solution.py:14
  119.1 1.4 copy.35
  120.6 2.2 gather_fusion.1
  122.8 1.5 fusion.19
  124.3 1.5 fusion.25
  125.9 0.7 gather_fusion.2
  126.6 1.9 convolution_convert_fusion.2
  128.5 0.2 broadcast.57
  128.7 3.5 %scatter_fusion.1 = bf16[64,100,128]{2,1,0:T(8,128)(2,1)S(1)} fusion(bf16[64,100,128]{2,1,0:T(8,128)(2,1)S(1)} %broadcast.57, s32[32]{0:T(128)S(1)} %get-tuple-element.10, bf16[32,100,128]{2,1,0:T(8,128)(2,1)} %convolution_convert_fusion.2), kind=kCustom, calls=%fused_computation.6 | custom fusion | bytes 2457728 | tf_op jit(solution)/shard_map/scatter | solution.py:53
  132.2 1.3 copy.38
  133.5 42.1 %all_to_all.29 = bf16[32,2,100,128]{3,1,2,0:T(2,128)(2,1)S(1)} all-to-all(bf16[32,2,100,128]{3,1,2,0:T(2,128)(2,1)S(1)} %copy.38), channel_id=1, replica_groups=mesh['ice'=4,'ocn'=8] {'ice','ocn'}, dimensions={0} | all-to-all | bytes 3276800 | tf_op jit(solution)/shard_map/all_to_all | solution.py:10
  175.6 1.8 copy.39
  177.4 0.3 convolution_bitcast_fusion
  177.7 0.6 convolution_convert_fusion
  178.4 2.3 %copy.40 = bf16[32,2,100,128]{3,1,2,0:T(2,128)(2,1)} copy(bf16[32,2,100,128]{3,1,0,2:T(2,128)(2,1)S(1)} %bitcast.69) | data formatting | bytes 3276800 | tf_op jit(solution)/shard_map/reshape | solution.py:65
  180.7 2.8 %all-to-all-start.4 = ((bf16[32,2,100,128]{3,1,2,0:T(2,128)(2,1)}), bf16[32,2,100,128]{3,1,2,0:T(2,128)(2,1)S(1)}, u32[]{:S(2)}, u32[]{:S(2)}) async-start(bf16[32,2,100,128]{3,1,2,0:T(2,128)(2,1)} %copy.40), calls=%async_computation.4 | async-start | bytes 3276800 | tf_op jit(solution)/shard_map/all_to_all | solution.py:14
  183.6 0.8 tanh.36
  184.4 0.8 reshape.121
  185.2 1.9 tanh_convert_fusion
  187.1 36.7 %all-to-all-done.4 = bf16[32,2,100,128]{3,1,2,0:T(2,128)(2,1)S(1)} async-done(((bf16[32,2,100,128]{3,1,2,0:T(2,128)(2,1)}), bf16[32,2,100,128]{3,1,2,0:T(2,128)(2,1)S(1)}, u32[]{:S(2)}, u32[]{:S(2)}) %all-to-all-start.4) | async-done | bytes 1638432 | tf_op jit(solution)/shard_map/all_to_all | solution.py:14
  223.8 1.4 copy.41
  225.2 2.2 gather_fusion.3
  227.4 1.5 fusion.18
  228.9 0.8 fusion.10
  229.8 0.2 copy-done.1
  230.0 0.9 multiply_convert_fusion
  (18 shorter events, 0.5 us)
Async XLA Ops:
  0.6 13.8 %copy-start = (bf16[32,128,128]{2,1,0:T(8,128)(2,1)S(1)}, bf16[32,128,128]{2,1,0:T(8,128)(2,1)}, u32[]{:S(2)}) copy-start(bf16[32,128,128]{2,1,0:T(8,128)(2,1)} %param.11) | copy-start | bytes 3145732
  3.7 18.8 %all-to-all-start = ((s32[32,1,2]{2,1,0:T(1,128)}), s32[32,1,2]{2,1,0:T(1,128)S(1)}, u32[]{:S(2)}, u32[]{:S(2)}) async-start(s32[32,1,2]{2,1,0:T(1,128)} %bitcast.4), calls=%async_computation | async-start | bytes 32768 | tf_op jit(solution)/shard_map/all_to_all | solution.py:37
  22.5 46.1 %all-to-all-start.1 = ((bf16[32,2,100,128]{3,1,2,0:T(2,128)(2,1)}), bf16[32,2,100,128]{3,1,2,0:T(2,128)(2,1)S(1)}, u32[]{:S(2)}, u32[]{:S(2)}) async-start(bf16[32,2,100,128]{3,1,2,0:T(2,128)(2,1)} %copy.32), calls=%async_computation.1 | async-start | bytes 3276800 | tf_op jit(solution)/shard_map/all_to_all | solution.py:10
  76.1 2.8 %copy-start.4 = (f32[5,20]{1,0:T(8,128)S(1)}, f32[5,20]{1,0:T(8,128)}, u32[]{:S(2)}) copy-start(f32[5,20]{1,0:T(8,128)} %param.10) | copy-start | bytes 1204
  76.1 43.0 %all-to-all-start.2 = ((bf16[32,2,100,128]{3,1,2,0:T(2,128)(2,1)}), bf16[32,2,100,128]{3,1,2,0:T(2,128)(2,1)S(1)}, u32[]{:S(2)}, u32[]{:S(2)}) async-start(bf16[32,2,100,128]{3,1,2,0:T(2,128)(2,1)} %copy.34), calls=%async_computation.2 | async-start | bytes 3276800 | tf_op jit(solution)/shard_map/all_to_all | solution.py:14
  180.7 2.8 %copy-start.2 = (f32[100,128,8]{1,2,0:T(8,128)S(1)}, f32[100,128,8]{1,2,0:T(8,128)}, u32[]{:S(2)}) copy-start(f32[100,128,8]{1,2,0:T(8,128)} %get-tuple-element.9) | copy-start | bytes 1228804
  180.7 43.0 %all-to-all-start.4 = ((bf16[32,2,100,128]{3,1,2,0:T(2,128)(2,1)}), bf16[32,2,100,128]{3,1,2,0:T(2,128)(2,1)S(1)}, u32[]{:S(2)}, u32[]{:S(2)}) async-start(bf16[32,2,100,128]{3,1,2,0:T(2,128)(2,1)} %copy.40), calls=%async_computation.4 | async-start | bytes 3276800 | tf_op jit(solution)/shard_map/all_to_all | solution.py:14
  228.9 1.0 copy-start.1
  228.9 1.1 copy-start.3
where the time goes:
time: 232 us; the launch traced here: 231 us
  waiting for transfers between devices  115 us (50%)
  blocking collectives  42.1 us (18%)
  local copies, waits for them, and re-layouts  34.7 us (15%)
  starting transfers between devices  18.8 us (8%)
  matrix products  12.2 us (5%)
  other arithmetic  7.61 us (3%)
    all_to_all x2, waiting for transfers between devices, back_move(): lax.all_to_all(buffer, ('ice', 'ocn'), split_axis=0, concat_axis=0, tiled...  76.8 us
    all_to_all x1, blocking collectives, forward_move(): lax.all_to_all(buffer, ('ice', 'ocn'), split_axis=0, concat_axis=0, tiled...  42.1 us
    all_to_all x1, waiting for transfers between devices, forward_move(): lax.all_to_all(buffer, ('ice', 'ocn'), split_axis=0, concat_axis=0, tiled...  37.8 us
    all_to_all x1, starting transfers between devices, on_device(): lax.all_to_all(meta_send, ('ice', 'ocn'), split_axis=0, concat_axis=0, ti...  7.33 us
    scatter x2, local copies, waits for them, and re-layouts, on_device(): jnp.zeros((devices * CAP, chans, width), jnp.bfloat16).at[place].set(prods)  7.06 us
    all_to_all x1, starting transfers between devices, forward_move(): lax.all_to_all(buffer, ('ice', 'ocn'), split_axis=0, concat_axis=0, tiled...  5.83 us
    all_to_all x2, starting transfers between devices, back_move(): lax.all_to_all(buffer, ('ice', 'ocn'), split_axis=0, concat_axis=0, tiled...  5.64 us
    all_to_all x2, local copies, waits for them, and re-layouts, forward_move(): lax.all_to_all(buffer, ('ice', 'ocn'), split_axis=0, concat_axis=0, tiled...  4.85 us
  transfers between devices with their start and end apart: 4, of which 3 were waited for; matrix products, arithmetic and copies ran while one was open for 8% of the time, Pallas kernels for 0%

commit v1 on v0

v1 whole, which is shorter than its diff:
```python
import functools

import jax
import jax.numpy as jnp
from jax import lax
from jax.experimental import pallas as pl
from jax.experimental.pallas import tpu as pltpu
from jax.sharding import PartitionSpec as P

CAP = 2
AXES = ("ice", "ocn")
LINE = 4
ROWS = 16


def spread(first, count):
    return sorted(range(first, count), key=lambda c: min(c, count - c))


def kernel(
    sizes, blk_ref, tile_ref, meta_ref, ohf_ref, ohb_ref,
    ice_in, ocean_ref, rate_ref, land_ref, w_ref,
    ice_ref, flux_out,
    psend, prec, zsend, zrec, frec, bsend, ret, contrib, total,
    ps_s, ps_r, zs_s, zs_r, fs_s, fs_r, bs_s, bs_r,
):
    Z, Y, N, tiles = sizes
    chans, width = ice_in.shape[1:]
    per = N * CAP
    steps = chans // ROWS
    ice_id, ocn_id = lax.axis_index("ice"), lax.axis_index("ocn")
    z, y = ocn_id // Y, ocn_id % Y
    p = ice_id * Y + y

    def plane(j):
        q = (p + j) % N
        return {"ice": q // Y, "ocn": z * Y + q % Y}

    def line(c):
        return {"ice": ice_id, "ocn": ((z + c) % Z) * Y + y}

    barrier = pltpu.get_barrier_semaphore()
    for j in range(1, N):
        pl.semaphore_signal(barrier, inc=1, device_id=plane(j), device_id_type=pl.DeviceIdType.MESH)
    for c in range(1, Z):
        pl.semaphore_signal(barrier, inc=1, device_id=line(c), device_id_type=pl.DeviceIdType.MESH)
    pl.semaphore_wait(barrier, N - 1 + Z - 1)

    def remote(src, dst, s, r, dev):
        return pltpu.make_async_remote_copy(
            src_ref=src, dst_ref=dst, send_sem=s, recv_sem=r,
            device_id=dev, device_id_type=pl.DeviceIdType.MESH,
        )

    def pcopy(c, j):
        at = pl.ds((c * N + j) * CAP, CAP)
        return remote(psend.at[at], prec.at[at], ps_s.at[c, j], ps_r.at[c, j], plane(j))

    def bcopy(c, j):
        at = pl.ds((c * N + j) * CAP, CAP)
        return remote(bsend.at[at], ret.at[at], bs_s.at[c, j], bs_r.at[c, j], plane(N - j))

    def zcopy(c):
        return remote(zsend.at[c], zrec.at[c], zs_s.at[c], zs_r.at[c], line(c))

    def fcopy(c):
        return remote(frec[0], frec[c], fs_s.at[c], fs_r.at[c], line(c))

    def gather(load, weights, base, start, finish):
        def rows(r, carry):
            at = pl.ds(pl.multiple_of(r * ROWS, ROWS), ROWS)

            def add(k, accs):
                x = load(k, at)
                return tuple(
                    accs[t] + weights[(base + k) * tiles + t] * x for t in range(tiles)
                )

            accs = lax.fori_loop(0, per, add, tuple(start(t, at) for t in range(tiles)), unroll=True)
            for t in range(tiles):
                finish(t, at, accs[t])
            return carry

        lax.fori_loop(0, steps, rows, 0)

    ice_ref[...] = ice_in[...]
    near = spread(1, Z)

    def turn(number, carry):
        for c in near[::-1] + [0]:
            for n in range(per):
                slot = c * per + n
                block = blk_ref[slot]
                prod = jnp.dot(
                    ice_ref[tile_ref[slot]], w_ref[block], preferred_element_type=jnp.float32
                ).astype(jnp.bfloat16)
                if n < CAP:
                    prec[slot] = prod
                else:
                    psend[slot] = prod
            for j in range(1, N):
                pcopy(c, j).start()
        for c in near[::-1] + [0]:
            for j in range(1, N):
                pcopy(c, j).wait_recv()
            base = c * per

            def load(k, at):
                return prec[base + k, at, :].astype(jnp.float32)

            def start(t, at):
                return jnp.zeros((ROWS, width), jnp.float32)

            def finish(t, at, acc):
                if c == 0:
                    total[t, at, :] = acc
                else:
                    zsend[c, t, at, :] = acc.astype(jnp.bfloat16)

            gather(load, ohf_ref, base, start, finish)
            if c:
                zcopy(c).start()
        for c in near:
            zcopy(c).wait_recv()

        def flux_rows(r, carry):
            at = pl.ds(pl.multiple_of(r * ROWS, ROWS), ROWS)
            for t in range(tiles):
                acc = total[t, at, :]
                for c in near:
                    acc = acc + zrec[c, t, at, :].astype(jnp.float32)
                acc = jnp.tanh(acc + ocean_ref[t, at, :].astype(jnp.float32))
                frec[0][t, at, :] = acc.astype(jnp.bfloat16)
                total[t, at, :] = jnp.zeros((ROWS, width), jnp.float32)
            return carry

        lax.fori_loop(0, steps, flux_rows, 0)
        for c in near:
            fcopy(c).start()
        for c in [0] + near:
            held = (Z - c) % Z
            if c:
                fcopy(held).wait_recv()
            for n in range(per):
                slot = c * per + n
                tile = frec[held][meta_ref[slot]]
                if n < CAP:
                    ret[slot] = tile
                else:
                    bsend[slot] = tile
            for j in range(1, N):
                bcopy(c, j).start()
        for c in [0] + near:
            for j in range(1, N):
                bcopy(c, j).wait_recv()
            base = c * per
            for n in range(per):
                contrib[n] = lax.dot_general(
                    ret[base + n], w_ref[blk_ref[base + n]], (((1,), (1,)), ((), ())),
                    preferred_element_type=jnp.float32,
                )

            def load(k, at):
                return contrib[k, at, :]

            def start(t, at):
                return total[t, at, :]

            def finish(t, at, acc):
                total[t, at, :] = acc

            gather(load, ohb_ref, base, start, finish)

        def ice_rows(r, carry):
            at = pl.ds(pl.multiple_of(r * ROWS, ROWS), ROWS)
            rate = rate_ref[at, :]
            for t in range(tiles):
                old = ice_ref[t, at, :].astype(jnp.float32)
                new = land_ref[pl.ds(t, 1), :] * (old + rate * jnp.tanh(total[t, at, :]))
                ice_ref[t, at, :] = new.astype(jnp.bfloat16)
            return carry

        lax.fori_loop(0, steps, ice_rows, 0)
        for c in range(Z):
            for j in range(1, N):
                pcopy(c, j).wait_send()
                bcopy(c, j).wait_send()
        for c in near:
            zcopy(c).wait_send()
            fcopy(c).wait_send()
        return carry

    lax.fori_loop(0, 2, turn, 0)
    flux_out[...] = frec[0][...]


def on_device(
    ice_state, ocean_state, ice_rate, block_weights, block_route, block_tiles, block_valid, ice_mask
):
    cats, fields, cells = ice_state.shape
    chans = cats * fields
    rows = -(-chans // ROWS) * ROWS
    blocks, width, unused = block_weights.shape
    tiles = cells // width
    outer = lax.axis_size("ocn")
    Z = LINE if outer % LINE == 0 else outer
    Y = outer // Z
    N = lax.axis_size("ice") * Y
    ice_id, ocn_id = lax.axis_index("ice"), lax.axis_index("ocn")
    z, y = ocn_id // Y, ocn_id % Y
    p = ice_id * Y + y

    def number(q, zz):
        return ((q // Y) * outer + zz * Y + q % Y).astype(jnp.int32)

    route = block_route[:, 0]
    source, target = block_tiles[:, 0], block_tiles[:, 1]
    order = jnp.arange(blocks, dtype=jnp.int32)
    earlier = (route[None, :] == route[:, None]) & (order[None, :] < order[:, None])
    slot = jnp.sum(earlier.astype(jnp.int32), axis=1)
    gathered = lax.all_gather((route * tiles + target) * CAP + slot, AXES, axis=0, tiled=False)
    gathered = gathered.reshape(-1, blocks)

    js = jnp.arange(N, dtype=jnp.int32)
    cs = jnp.arange(Z, dtype=jnp.int32)
    ks = jnp.arange(CAP, dtype=jnp.int32)
    ts = jnp.arange(tiles, dtype=jnp.int32)
    dest = number((p + js)[None, :] % N, ((z + cs) % Z)[:, None])
    code = route * CAP + slot
    sel = code == (dest[:, :, None] * CAP + ks)[..., None]
    blk = jnp.sum(jnp.where(sel, order, 0), axis=-1).reshape(-1)
    src = jnp.sum(jnp.where(sel, source, 0), axis=-1).reshape(-1)
    some = jnp.any(sel, axis=-1).reshape(-1)
    ohb = ((src[:, None] == ts) & some[:, None]).astype(jnp.float32).reshape(-1)
    theirs = gathered[number((p - js) % N, z)]
    key = (theirs // (tiles * CAP)) * CAP + theirs % CAP
    own = number(p, (z + cs) % Z)
    rsel = key[None, :, None, :] == (own[:, None] * CAP + ks)[:, None, :, None]
    meta = jnp.sum(jnp.where(rsel, ((theirs // CAP) % tiles)[None, :, None, :], 0), axis=-1).reshape(-1)
    rsome = jnp.any(rsel, axis=-1).reshape(-1)
    ohf = ((meta[:, None] == ts) & rsome[:, None]).astype(jnp.float32).reshape(-1)

    live = jnp.arange(width, dtype=jnp.int32)[None, :] < block_valid[:, None]
    masked = jnp.where(live[:, :, None], block_weights, jnp.zeros((), jnp.bfloat16))

    def tiled(values):
        values = values.reshape(chans, tiles, width).transpose(1, 0, 2)
        return jnp.pad(values, ((0, 0), (0, rows - chans), (0, 0)))

    ice = tiled(ice_state * ice_mask.astype(jnp.bfloat16)[None, None, :])
    ocean = tiled(ocean_state)
    rates = jnp.broadcast_to(jnp.pad(ice_rate.reshape(chans, 1), ((0, rows - chans), (0, 0))), (rows, width))
    land = ice_mask.astype(jnp.float32).reshape(tiles, width)
    slots = Z * N * CAP
    smem, vmem = pl.BlockSpec(memory_space=pltpu.SMEM), pl.BlockSpec(memory_space=pltpu.VMEM)
    tile = (rows, width)
    ice, flux = pl.pallas_call(
        functools.partial(kernel, (Z, Y, N, tiles)),
        out_shape=(jax.ShapeDtypeStruct((tiles,) + tile, jnp.bfloat16),) * 2,
        in_specs=[smem] * 5 + [vmem] * 5,
        out_specs=(vmem, vmem),
        scratch_shapes=[
            pltpu.VMEM((slots,) + tile, jnp.bfloat16),
            pltpu.VMEM((slots,) + tile, jnp.bfloat16),
            pltpu.VMEM((Z, tiles) + tile, jnp.bfloat16),
            pltpu.VMEM((Z, tiles) + tile, jnp.bfloat16),
            tuple(pltpu.VMEM((tiles,) + tile, jnp.bfloat16) for c in range(Z)),
            pltpu.VMEM((slots,) + tile, jnp.bfloat16),
            pltpu.VMEM((slots,) + tile, jnp.bfloat16),
            pltpu.VMEM((N * CAP,) + tile, jnp.float32),
            pltpu.VMEM((tiles,) + tile, jnp.float32),
            pltpu.SemaphoreType.DMA((Z, N)),
            pltpu.SemaphoreType.DMA((Z, N)),
            pltpu.SemaphoreType.DMA((Z,)),
            pltpu.SemaphoreType.DMA((Z,)),
            pltpu.SemaphoreType.DMA((Z,)),
            pltpu.SemaphoreType.DMA((Z,)),
            pltpu.SemaphoreType.DMA((Z, N)),
            pltpu.SemaphoreType.DMA((Z, N)),
        ],
        compiler_params=pltpu.CompilerParams(
            collective_id=0, has_side_effects=True, vmem_limit_bytes=60 * 1024 * 1024
        ),
    )(blk, src, meta, ohf, ohb, ice, ocean, rates, land, masked)

    def flat(values):
        return values[:, :chans].transpose(1, 0, 2).reshape(cats, fields, cells)

    return flat(ice), flat(flux)


def solution(mesh):
    placed = (
        P(None, None, ("ice", "ocn")),
        P(None, None, ("ice", "ocn")),
        P(),
        P(("ice", "ocn"), None, None),
        P(("ice", "ocn"), None),
        P(("ice", "ocn"), None),
        P(("ice", "ocn")),
        P(("ice", "ocn")),
    )
    return jax.shard_map(
        on_device,
        mesh=mesh,
        in_specs=placed,
        out_specs=(P(None, None, ("ice", "ocn")), P(None, None, ("ice", "ocn"))),
        check_vma=False,
    )
```

time: 232 us -> 211 us (0.909)
  Pallas kernels: 0 us -> 126 us
  waiting for transfers between devices: 115 us -> 0 us
  blocking collectives: 42.1 us -> 69.8 us
  local copies, waits for them, and re-layouts: 34.7 us -> 10.5 us
  starting transfers between devices: 18.8 us -> 0 us
  matrix products: 12.2 us -> 0 us
  other arithmetic: 7.61 us -> 4.09 us
    pallas_call x0 -> x1, Pallas kernels: none -> 126 us  [on_device(): pl.pallas_call(functools.partial(kernel, (Z, Y, N, tiles)), out_shape=(ja...]
    all_to_all x4 -> x0, waiting for transfers between devices: 115 us -> none  [the longest x2 76.8 us: back_move(): lax.all_to_all(buffer, ('ice', 'ocn'), split_axis=0, concat_axis=0, tiled...]
    all_gather x0 -> x1, blocking collectives: none -> 69.8 us  [on_device(): lax.all_gather((route * tiles + target) * CAP + slot, AXES, axis=0, tiled...]
    all_to_all x1 -> x0, blocking collectives: 42.1 us -> none  [forward_move(): lax.all_to_all(buffer, ('ice', 'ocn'), split_axis=0, concat_axis=0, tiled...]
    all_to_all x4 -> x0, starting transfers between devices: 18.8 us -> none  [the longest x1 7.33 us: on_device(): lax.all_to_all(meta_send, ('ice', 'ocn'), split_axis=0, concat_axis=0, ti...]
    dot_general x9 -> x0, matrix products: 12.2 us -> none  [the longest x2 3.73 us: on_device(): jnp.einsum('cbi,bio->bco', picked, masked, preferred_element_type=jnp.flo...]
    all_to_all x6 -> x0, local copies, waits for them, and re-layouts: 8.94 us -> none  [the longest x2 4.85 us: forward_move(): lax.all_to_all(buffer, ('ice', 'ocn'), split_axis=0, concat_axis=0, tiled...]
    scatter x3 -> x0, local copies, waits for them, and re-layouts: 7.73 us -> none  [the longest x2 7.06 us: on_device(): jnp.zeros((devices * CAP, chans, width), jnp.bfloat16).at[place].set(prods)]
  transfers between devices with their start and end apart: 4 -> 0, of which waited for: 3 -> 0; matrix products, arithmetic and copies ran while one was open for 8% -> 0% of each run, Pallas kernels for 0% -> 0%
where the time goes in v1:
time: 211 us
  Pallas kernels  126 us (60%)
  blocking collectives  69.8 us (33%)
  local copies, waits for them, and re-layouts  10.5 us (5%)
  other arithmetic  4.09 us (2%)
    pallas_call x1, Pallas kernels, on_device(): pl.pallas_call(functools.partial(kernel, (Z, Y, N, tiles)), out_shape=(ja...  126 us
    all_gather x1, blocking collectives, on_device(): lax.all_gather((route * tiles + target) * CAP + slot, AXES, axis=0, tiled...  69.8 us

profile of v1, /device:TPU:0, one launch (start us, length us, event | category | flops | bytes accessed | tf_op | source)
XLA Modules:
  0.0 211.1 jit_solution(10301450875351572549)
XLA Ops:
  0.7 0.0 copy-start.9
  0.7 0.0 copy-start.6
  0.8 0.6 copy-done.9
  1.4 0.2 convert_reduce_fusion
  1.6 0.7 copy-done.10
  2.2 0.0 copy-done.6
  2.2 0.1 reshape.460
  2.3 0.0 copy-start.1
  2.4 0.1 add_multiply_fusion
  2.4 0.1 iota_add_fusion.1
  2.5 0.3 compare_reduce_fusion
  2.8 0.1 copy.24
  2.9 0.1 and.227
  3.0 0.4 fusion.2
  3.5 0.1 iota_compare_fusion.2
  3.6 0.0 copy-done.7
  3.6 0.6 convert_bitcast_fusion
  4.2 0.1 copy.21
  4.3 0.1 reshape.456.tile_ref
  4.4 69.8 %all-gather = s32[32,1,32]{2,1,0:T(1,128)S(1)} all-gather(s32[1,1,32]{2,1,0:T(1,128)S(1)} %fusion.20), channel_id=1, replica_groups=mesh['ice'=4,'ocn'=8] {'ice','ocn'}, dimensions={0}, use_global_device_ids=true | all-gather | bytes 4224 | tf_op jit(solution)/shard_map/all_gather | solution.py:221
  74.2 0.6 gather_fusion
  74.7 0.3 fusion
  75.0 0.3 compare_reduce_fusion.1
  75.3 0.1 copy.23
  75.4 0.1 and.224
  75.6 0.1 copy.22
  75.7 0.1 reshape.457.meta_ref
  75.8 0.1 copy.20
  75.9 0.7 reshape.455.blk_ref
  76.6 0.1 fusion.4
  76.7 0.7 reshape.464.ohf_ref
  77.3 0.1 fusion.6
  77.4 0.7 reshape.465.ohb_ref
  78.1 0.7 broadcast_in_dim.66.rate_ref
  78.8 0.0 copy-done.1
  78.8 0.1 reshape.459
  78.9 0.0 copy-start.2
  79.0 0.0 copy-start
  79.0 0.7 pad.12.ocean_ref
  79.7 0.3 copy-done.2
  80.0 0.1 reshape.458
  80.2 0.7 pad.11.ice_in
  80.9 1.5 broadcast_select_fusion.w_ref
  82.4 125.9 %shard_map.95 = (bf16[8,112,128]{2,1,0:T(8,128)(2,1)}, bf16[8,112,128]{2,1,0:T(8,128)(2,1)}) custom-call(s32[64]{0:T(128)} %reshape.455.blk_ref, s32[64]{0:T(128)} %copy-done.4, s32[64]{0:T(128)} %copy-done.5, f32[512]{0:T(512)} %reshape.464.ohf_ref, f32[512]{0:T(512)} %reshape.465.ohb_ref, bf16[8,112,128]{2,1,0:T(8,128)(2,1)} %pad.11.ice_in, ...), custom_call_target="tpu_custom_call" | custom-call | tf_op jit(solution)/shard_map/pallas_call | solution.py:257
  208.3 1.0 slice_bitcast_fusion.1
  209.3 0.8 reshape.462
  210.1 0.1 copy-done.3
  210.3 0.8 reshape.463
  (26 shorter events, 0.3 us)
Async XLA Ops:
  0.7 0.7 copy-start.9
  0.7 1.5 copy-start.6
  1.5 0.7 copy-start.10
  2.3 1.2 copy-start.8
  2.3 1.3 copy-start.7
  2.3 76.5 %copy-start.1 = (bf16[5,20,1024]{2,1,0:T(8,128)(2,1)S(1)}, bf16[5,20,1024]{2,1,0:T(8,128)(2,1)}, u32[]{:S(2)}) copy-start(bf16[5,20,1024]{2,1,0:T(8,128)(2,1)} %param.9) | copy-start | bytes 614404
  4.4 72.9 %copy-start.4 = (s32[64]{0:T(128)}, s32[64]{0:T(128)S(1)}, u32[]{:S(2)}) copy-start(s32[64]{0:T(128)S(1)} %reshape.456.tile_ref) | copy-start | bytes 772
  75.8 0.8 copy-start.5
  78.9 1.0 copy-start.2
  79.0 1.9 copy-start
  209.3 0.9 copy-start.3

commit v2 on v1

--- a/solution.py
+++ b/solution.py
@@ -18,10 +18,11 @@
 
 
 def kernel(
-    sizes, blk_ref, tile_ref, meta_ref, ohf_ref, ohb_ref,
+    sizes, blk_ref, tile_ref, names_ref,
     ice_in, ocean_ref, rate_ref, land_ref, w_ref,
     ice_ref, flux_out,
-    psend, prec, zsend, zrec, frec, bsend, ret, contrib, total,
+    names_in, names, psend, prec, zsend, zrec, frec, bsend, ret, contrib, total,
+    ns_s, ns_r, nl,
     ps_s, ps_r, zs_s, zs_r, fs_s, fs_r, bs_s, bs_r,
 ):
     Z, Y, N, tiles = sizes
@@ -66,15 +67,28 @@
     def fcopy(c):
         return remote(frec[0], frec[c], fs_s.at[c], fs_r.at[c], line(c))
 
-    def gather(load, weights, base, start, finish):
+    def ncopy(j):
+        return remote(names_ref.at[j], names_in.at[j], ns_s.at[j], ns_r.at[j], plane(j))
+
+    def nlocal(j):
+        held = names_in if j else names_ref
+        return pltpu.make_async_copy(held.at[j], names.at[j], nl.at[j])
+
+    def name(c, n):
+        return names[n // CAP, 0, c * CAP + n % CAP]
+
+    for j in range(1, N):
+        ncopy(j).start()
+    nlocal(0).start()
+
+    def gather(load, place, start, finish):
         def rows(r, carry):
             at = pl.ds(pl.multiple_of(r * ROWS, ROWS), ROWS)
 
             def add(k, accs):
                 x = load(k, at)
-                return tuple(
-                    accs[t] + weights[(base + k) * tiles + t] * x for t in range(tiles)
-                )
+                to = jnp.full((ROWS, width), place(k), jnp.int32)
+                return tuple(accs[t] + jnp.where(to == t, x, 0.0) for t in range(tiles))
 
             accs = lax.fori_loop(0, per, add, tuple(start(t, at) for t in range(tiles)), unroll=True)
             for t in range(tiles):
@@ -85,6 +99,11 @@
 
     ice_ref[...] = ice_in[...]
     near = spread(1, Z)
+    for j in range(1, N):
+        ncopy(j).wait_recv()
+        nlocal(j).start()
+    for j in range(N):
+        nlocal(j).wait()
 
     def turn(number, carry):
         for c in near[::-1] + [0]:
@@ -92,7 +111,7 @@
                 slot = c * per + n
                 block = blk_ref[slot]
                 prod = jnp.dot(
-                    ice_ref[tile_ref[slot]], w_ref[block], preferred_element_type=jnp.float32
+                    ice_ref[tile_ref[slot] % tiles], w_ref[block], preferred_element_type=jnp.float32
                 ).astype(jnp.bfloat16)
                 if n < CAP:
                     prec[slot] = prod
@@ -117,7 +136,7 @@
                 else:
                     zsend[c, t, at, :] = acc.astype(jnp.bfloat16)
 
-            gather(load, ohf_ref, base, start, finish)
+            gather(load, lambda k: name(c, k), start, finish)
             if c:
                 zcopy(c).start()
         for c in near:
@@ -143,7 +162,7 @@
                 fcopy(held).wait_recv()
             for n in range(per):
                 slot = c * per + n
-                tile = frec[held][meta_ref[slot]]
+                tile = frec[held][name(c, n) % tiles]
                 if n < CAP:
                     ret[slot] = tile
                 else:
@@ -169,7 +188,7 @@
             def finish(t, at, acc):
                 total[t, at, :] = acc
 
-            gather(load, ohb_ref, base, start, finish)
+            gather(load, lambda k: tile_ref[base + k], start, finish)
 
         def ice_rows(r, carry):
             at = pl.ds(pl.multiple_of(r * ROWS, ROWS), ROWS)
@@ -192,6 +211,8 @@
 
     lax.fori_loop(0, 2, turn, 0)
     flux_out[...] = frec[0][...]
+    for j in range(1, N):
+        ncopy(j).wait_send()
 
 
 def on_device(
@@ -218,28 +239,17 @@
     order = jnp.arange(blocks, dtype=jnp.int32)
     earlier = (route[None, :] == route[:, None]) & (order[None, :] < order[:, None])
     slot = jnp.sum(earlier.astype(jnp.int32), axis=1)
-    gathered = lax.all_gather((route * tiles + target) * CAP + slot, AXES, axis=0, tiled=False)
-    gathered = gathered.reshape(-1, blocks)
-
     js = jnp.arange(N, dtype=jnp.int32)
     cs = jnp.arange(Z, dtype=jnp.int32)
     ks = jnp.arange(CAP, dtype=jnp.int32)
-    ts = jnp.arange(tiles, dtype=jnp.int32)
     dest = number((p + js)[None, :] % N, ((z + cs) % Z)[:, None])
     code = route * CAP + slot
     sel = code == (dest[:, :, None] * CAP + ks)[..., None]
     blk = jnp.sum(jnp.where(sel, order, 0), axis=-1).reshape(-1)
-    src = jnp.sum(jnp.where(sel, source, 0), axis=-1).reshape(-1)
-    some = jnp.any(sel, axis=-1).reshape(-1)
-    ohb = ((src[:, None] == ts) & some[:, None]).astype(jnp.float32).reshape(-1)
-    theirs = gathered[number((p - js) % N, z)]
-    key = (theirs // (tiles * CAP)) * CAP + theirs % CAP
-    own = number(p, (z + cs) % Z)
-    rsel = key[None, :, None, :] == (own[:, None] * CAP + ks)[:, None, :, None]
-    meta = jnp.sum(jnp.where(rsel, ((theirs // CAP) % tiles)[None, :, None, :], 0), axis=-1).reshape(-1)
-    rsome = jnp.any(rsel, axis=-1).reshape(-1)
-    ohf = ((meta[:, None] == ts) & rsome[:, None]).astype(jnp.float32).reshape(-1)
-
+    src = tiles + jnp.sum(jnp.where(sel, source - tiles, 0), axis=-1).reshape(-1)
+    names = tiles + jnp.sum(jnp.where(sel, target - tiles, 0), axis=-1)
+    names = names.transpose(1, 0, 2).reshape(N, 1, Z * CAP)
+    names = jnp.pad(names, ((0, 0), (0, 0), (0, width - Z * CAP)))
     live = jnp.arange(width, dtype=jnp.int32)[None, :] < block_valid[:, None]
     masked = jnp.where(live[:, :, None], block_weights, jnp.zeros((), jnp.bfloat16))
 
@@ -257,9 +267,11 @@
     ice, flux = pl.pallas_call(
         functools.partial(kernel, (Z, Y, N, tiles)),
         out_shape=(jax.ShapeDtypeStruct((tiles,) + tile, jnp.bfloat16),) * 2,
-        in_specs=[smem] * 5 + [vmem] * 5,
+        in_specs=[smem] * 2 + [vmem] * 6,
         out_specs=(vmem, vmem),
         scratch_shapes=[
+            pltpu.VMEM((N, 1, width), jnp.int32),
+            pltpu.SMEM((N, 1, width), jnp.int32),
             pltpu.VMEM((slots,) + tile, jnp.bfloat16),
             pltpu.VMEM((slots,) + tile, jnp.bfloat16),
             pltpu.VMEM((Z, tiles) + tile, jnp.bfloat16),
@@ -269,6 +281,9 @@
             pltpu.VMEM((slots,) + tile, jnp.bfloat16),
             pltpu.VMEM((N * CAP,) + tile, jnp.float32),
             pltpu.VMEM((tiles,) + tile, jnp.float32),
+            pltpu.SemaphoreType.DMA((N,)),
+            pltpu.SemaphoreType.DMA((N,)),
+            pltpu.SemaphoreType.DMA((N,)),
             pltpu.SemaphoreType.DMA((Z, N)),
             pltpu.SemaphoreType.DMA((Z, N)),
             pltpu.SemaphoreType.DMA((Z,)),
@@ -281,7 +296,7 @@
         compiler_params=pltpu.CompilerParams(
             collective_id=0, has_side_effects=True, vmem_limit_bytes=60 * 1024 * 1024
         ),
-    )(blk, src, meta, ohf, ohb, ice, ocean, rates, land, masked)
+    )(blk, src, names, ice, ocean, rates, land, masked)
 
     def flat(values):
         return values[:, :chans].transpose(1, 0, 2).reshape(cats, fields, cells)

time: 211 us -> 148 us (0.70)
  blocking collectives: 69.8 us -> 0 us
  Pallas kernels: 126 us -> 132 us
  other arithmetic: 4.09 us -> 6.63 us
    all_gather x1 -> x0, blocking collectives: 69.8 us -> none  [on_device(): lax.all_gather((route * tiles + target) * CAP + slot, AXES, axis=0, tiled...]
    pallas_call x1, Pallas kernels: 126 us -> 132 us  [on_device(): pl.pallas_call(functools.partial(kernel, (Z, Y, N, tiles)), out_shape=(ja...]
where the time goes in v2:
time: 148 us
  Pallas kernels  132 us (89%)
  local copies, waits for them, and re-layouts  8.58 us (6%)
  other arithmetic  6.63 us (4%)
    pallas_call x1, Pallas kernels, on_device(): pl.pallas_call(functools.partial(kernel, (Z, Y, N, tiles)), out_shape=(ja...  132 us

profile of v2, /device:TPU:0, one launch (start us, length us, event | category | flops | bytes accessed | tf_op | source)
XLA Modules:
  0.0 148.0 jit_solution(7341095885658850371)
XLA Ops:
  0.6 0.0 copy-start.1
  0.7 0.8 reshape.207
  1.5 0.9 convert_reduce_fusion
  2.4 0.7 multiply_add_fusion
  3.1 0.1 add_multiply_fusion
  3.2 0.8 add_bitcast_fusion.1
  4.0 0.7 iota_compare_fusion
  4.7 1.4 convert_bitcast_fusion
  6.0 0.6 fusion.2
  6.6 0.1 copy.20
  6.7 0.6 pad.15.names_ref
  7.3 0.1 copy.19
  7.4 0.7 add.171.tile_ref
  8.1 0.1 copy.18
  8.2 0.6 reshape.203.blk_ref
  8.8 0.7 broadcast_in_dim.52.rate_ref
  9.5 0.0 copy-done.1
  9.5 0.1 reshape.206
  9.7 0.0 copy-start.2
  9.7 0.0 copy-start
  9.7 0.7 pad.17.ocean_ref
  10.4 0.3 copy-done.2
  10.8 0.1 reshape.205
  10.9 0.7 pad.16.ice_in
  11.6 0.0 copy-done
  11.6 1.5 %broadcast_select_fusion.w_ref = bf16[32,128,128]{2,1,0:T(8,128)(2,1)} fusion(bf16[32,128,128]{2,1,0:T(8,128)(2,1)S(1)} %copy-done, pred[32,128]{1,0:T(8,128)(4,1)S(1)} %iota_compare_fusion), kind=kLoop, calls=%fused_computation | loop fusion | flops 524288 | bytes 2101248 | tf_op jit(solution)/shard_map/jit(_where)/select_n | solution.py:254
  13.2 132.0 %shard_map.95 = (bf16[8,112,128]{2,1,0:T(8,128)(2,1)}, bf16[8,112,128]{2,1,0:T(8,128)(2,1)}) custom-call(s32[64]{0:T(128)} %reshape.203.blk_ref, s32[64]{0:T(128)} %add.171.tile_ref, s32[8,1,128]{2,1,0:T(1,128)} %pad.15.names_ref, bf16[8,112,128]{2,1,0:T(8,128)(2,1)} %pad.16.ice_in, bf16[8,112,128]{2,1,0:T(8,128)(2,1)} %pad.17.ocean_ref, ...), custom_call_target="tpu_custom_call" | custom-call | tf_op jit(solution)/shard_map/pallas_call | solution.py:267
  145.2 1.0 slice_bitcast_fusion.1
  146.2 0.0 copy-start.3
  146.2 0.8 reshape.209
  147.0 0.1 copy-done.3
  147.2 0.8 reshape.210
  (12 shorter events, 0.2 us)
Async XLA Ops:
  0.6 8.9 %copy-start.1 = (bf16[5,20,1024]{2,1,0:T(8,128)(2,1)S(1)}, bf16[5,20,1024]{2,1,0:T(8,128)(2,1)}, u32[]{:S(2)}) copy-start(bf16[5,20,1024]{2,1,0:T(8,128)(2,1)} %param.9) | copy-start | bytes 614404
  9.7 1.0 copy-start.2
  9.7 1.9 %copy-start = (bf16[32,128,128]{2,1,0:T(8,128)(2,1)S(1)}, bf16[32,128,128]{2,1,0:T(8,128)(2,1)}, u32[]{:S(2)}) copy-start(bf16[32,128,128]{2,1,0:T(8,128)(2,1)} %param.11) | copy-start | bytes 3145732
  146.2 0.9 copy-start.3
